TPU v7x, 32 devices: a whole 2x2x4 slice. The times are simulated.
32 devices in a mesh: dp: 8 (over y, x, core), mp: 4 (over z).
Axes of the slice: x: 2, y: 2, z: 4, core: 2. Of those that a mesh axis runs over, the one named last changes fastest.
Arguments:
- tokens: bfloat16 [2048, 6144], P('dp', 'mp'), may hold values from -40 to 40
- norm_gain: float32 [6144], P('mp'), may hold values from 0.1 to 1.9
- w_qkv: bfloat16 [6144, 3, 4096], P('mp', None, 'dp'), may hold values from -0.078125 to 0.078125
- w_up: bfloat16 [6144, 12288], P('mp', 'dp'), may hold values from -0.078125 to 0.078125
- w_attn_out: bfloat16 [4096, 6144], P('dp', 'mp'), may hold values from -0.09375 to 0.09375
- w_down: bfloat16 [12288, 6144], P('dp', 'mp'), may hold values from -0.0546875 to 0.0546875
Outputs:
- layer_out: bfloat16 [2048, 6144], P('dp', 'mp')
All inputs are finite; a program needn't handle non-finite values.
Results may differ from a plain program's by a relative error of at most 0.015.
Values may be sent and summed in bfloat16 or wider, within the bound.
No kernel may reach another device: no remote copies, remote signals or barrier semaphores. Data moves between devices by JAX's collectives and lax.ppermute only.
A program may use at most 128 MiB of HBM per device.

v0:
```python
import jax
import jax.numpy as jnp
from jax import lax
from jax.sharding import PartitionSpec as P

HEAD_DIM = 128
PATCHES = 256


EPS = 1e-06


def normalize_rows(values, total, squares, gain, width):
    mean = total / width
    spread = squares / width - mean * mean
    scaled = (values - mean[:, None]) * lax.rsqrt(spread + EPS)[:, None]
    return (scaled * gain[None, :]).astype(jnp.bfloat16)


def head_norm(values):
    mean = jnp.mean(values, axis=-1, keepdims=True)
    centered = values - mean
    spread = jnp.mean(centered * centered, axis=-1, keepdims=True)
    return centered * lax.rsqrt(spread + EPS)


def attend(qkv, heads_here):
    rows = qkv.shape[0]
    images = rows // PATCHES
    parts = qkv.reshape(images, PATCHES, 3, heads_here, HEAD_DIM)
    query = (head_norm(parts[:, :, 0].astype(jnp.float32)) * (1.0 / HEAD_DIM) ** 0.5).astype(
        jnp.bfloat16
    )
    keys = head_norm(parts[:, :, 1].astype(jnp.float32)).astype(jnp.bfloat16)
    values = parts[:, :, 2]
    scores = jnp.einsum("iqhd,ikhd->ihqk", query, keys, preferred_element_type=jnp.float32)
    weights = jnp.exp(scores)
    probs = (weights / jnp.sum(weights, axis=-1, keepdims=True)).astype(jnp.bfloat16)
    mixed = jnp.einsum("ihqk,ikhd->iqhd", probs, values, preferred_element_type=jnp.float32)
    return mixed.astype(jnp.bfloat16).reshape(rows, heads_here * HEAD_DIM)


def local(tokens, norm_gain, w_qkv, w_up, w_attn_out, w_down):
    n_mp = lax.axis_size("mp")
    feat_here = tokens.shape[1]
    head_cols = w_qkv.shape[2]
    heads_here = head_cols // HEAD_DIM
    width = feat_here * n_mp
    tokens_f = tokens.astype(jnp.float32)
    total, squares = lax.psum(
        (jnp.sum(tokens_f, axis=1), jnp.sum(tokens_f * tokens_f, axis=1)), "mp"
    )
    normed = normalize_rows(tokens_f, total, squares, norm_gain, width)
    normed_all = lax.all_gather(normed, "dp", axis=0, tiled=True)
    w_heads = w_qkv.reshape(feat_here, 3 * head_cols)
    projected = lax.psum_scatter(
        jnp.concatenate(
            [
                jnp.dot(normed_all, w_heads, preferred_element_type=jnp.float32),
                jnp.dot(normed_all, w_up, preferred_element_type=jnp.float32),
            ],
            axis=1,
        ).astype(jnp.bfloat16),
        "mp",
        scatter_dimension=0,
        tiled=True,
    )
    qkv = projected[:, : 3 * head_cols].reshape(projected.shape[0], 3, head_cols)
    attended = attend(qkv, heads_here)
    activated = jax.nn.gelu(projected[:, 3 * head_cols :].astype(jnp.float32)).astype(jnp.bfloat16)
    hidden = jnp.concatenate([attended, activated], axis=1)
    piece = lax.all_gather(hidden, "mp", axis=0, tiled=True)
    result = jnp.dot(piece[:, :head_cols], w_attn_out, preferred_element_type=jnp.float32)
    partial_out = result + jnp.dot(piece[:, head_cols:], w_down, preferred_element_type=jnp.float32)
    summed = lax.psum_scatter(
        partial_out.astype(jnp.bfloat16), "dp", scatter_dimension=0, tiled=True
    ).astype(jnp.float32)
    return (tokens_f + summed).astype(jnp.bfloat16)


def solution(mesh):
    placed = (
        P("dp", "mp"),
        P("mp"),
        P("mp", None, "dp"),
        P("mp", "dp"),
        P("dp", "mp"),
        P("dp", "mp"),
    )
    return jax.shard_map(
        local, mesh=mesh, in_specs=placed, out_specs=P("dp", "mp"), check_vma=False
    )
```

profile of v0, /device:TPU:0, one launch (start us, length us, event | category | flops | bytes accessed | tf_op | source)
XLA Modules:
  0.0 583.7 jit_solution(13878567147038606246)
XLA Ops:
  6.5 0.0 copy-start
  6.5 0.0 all-gather.3.cloned.1.call-start
  6.5 1.6 convert_reduce_fusion
  8.1 13.5 %all-reduce = (f32[256]{0:T(256)S(1)}, f32[256]{0:T(256)S(1)}) all-reduce(f32[256]{0:T(256)S(1)} %get-tuple-element.6, f32[256]{0:T(256)S(1)} %get-tuple-element.5), channel_id=1, replica_groups=mesh['dp'=8,'mp'=4] {'mp'}, use_global_device_ids=true, to_apply=%region_3.0 | all-reduce | flops 512 | bytes 4096 | tf_op jit(solution)/shard_map/psum | solution.py:50
  21.6 2.3 fusion.11
  24.0 0.0 all-gather.3.cloned.1.call-update
  24.0 0.0 reduce-scatter.3.cloned.1.call-start
  24.0 6.8 %copy.12 = bf16[1536,3,512]{0,2,1:T(8,128)(2,1)} copy(bf16[1536,3,512]{2,0,1:T(8,128)(2,1)} %param.8) | data formatting | bytes 9437184 | tf_op args[2]
  30.8 36.9 %all-gather.3.cloned.1.call-done = bf16[2048,1536]{1,0:T(8,128)(2,1)} async-done(((bf16[256,1536]{1,0:T(8,128)(2,1)}), bf16[2048,1536]{1,0:T(8,128)(2,1)}) %all-gather.3.cloned.1.call-update) | async-done | bytes 6291472 | tf_op jit(solution)/shard_map/all_gather | solution.py:54
  67.7 13.5 %convolution_convert_fusion.1 = bf16[2048,1536]{0,1:T(8,128)(2,1)S(1)} fusion(bf16[2048,1536]{1,0:T(8,128)(2,1)} %all-gather.3.cloned.1.call-done, bf16[1536,1536]{0,1:T(8,128)(2,1)} %bitcast.51), kind=kOutput, calls=%fused_computation.3 | convolution fusion | flops 9666822144 | bytes 17301504 | tf_op jit(solution)/shard_map/dot_general | solution.py:59
  81.3 13.5 %convolution_convert_fusion = bf16[2048,1536]{0,1:T(8,128)(2,1)S(1)} fusion(bf16[2048,1536]{1,0:T(8,128)(2,1)} %all-gather.3.cloned.1.call-done, bf16[1536,1536]{1,0:T(8,128)(2,1)} %param.9), kind=kOutput, calls=%fused_computation.2 | convolution fusion | flops 9666822144 | bytes 17301504 | tf_op jit(solution)/shard_map/dot_general | solution.py:60
  94.8 14.5 %pad_maximum_fusion = bf16[2048,3072]{0,1:T(8,128)(2,1)} fusion(bf16[2048,1536]{0,1:T(8,128)(2,1)S(1)} %convolution_convert_fusion, bf16[2048,1536]{0,1:T(8,128)(2,1)S(1)} %convolution_convert_fusion.1), kind=kLoop, calls=%fused_computation | loop fusion | flops 25165824 | bytes 25165824 | tf_op jit(solution)/shard_map/concatenate | solution.py:57
  109.4 0.0 reduce-scatter.3.cloned.1.call-update
  109.4 0.2 all-gather.5.cloned.1.call-start
  109.6 211.8 %reduce-scatter.3.cloned.1.call-done = bf16[512,3072]{0,1:T(8,128)(2,1)} async-done(((bf16[2048,3072]{0,1:T(8,128)(2,1)}), bf16[512,3072]{0,1:T(8,128)(2,1)}) %reduce-scatter.3.cloned.1.call-update) | async-done | bytes 3145744 | tf_op jit(solution)/shard_map/reduce_scatter | solution.py:56
  321.4 2.7 slice.28
  324.1 2.4 reshape_reshape.3
  326.4 2.2 fusion.35
  328.6 1.4 copy.21
  330.0 0.2 convert_reduce_fusion.1
  330.2 0.0 copy-start.3
  330.2 0.7 fusion.24
  330.9 1.4 copy.20
  332.2 0.2 convert_reduce_fusion.2
  332.4 0.7 fusion.18
  333.1 2.8 exponential_reduce_fusion
  335.9 0.0 copy-done.3
  336.0 0.0 copy-start.2
  336.0 0.5 fusion.14
  336.5 0.5 copy.17
  337.0 0.1 copy.22
  337.1 0.7 copy-done.2
  337.8 1.1 fusion.6
  338.9 1.5 pad_maximum_fusion.1
  340.4 0.0 all-gather.5.cloned.1.call-update
  340.4 0.0 reduce-scatter.5.cloned.1.call-start
  340.5 150.8 %all-gather.5.cloned.1.call-done = bf16[2048,2048]{0,1:T(8,128)(2,1)} async-done(((bf16[512,2048]{0,1:T(8,128)(2,1)}), bf16[2048,2048]{0,1:T(8,128)(2,1)}) %all-gather.5.cloned.1.call-update) | async-done | bytes 8388624 | tf_op jit(solution)/shard_map/all_gather | solution.py:72
  491.3 0.0 copy-done
  491.3 0.0 copy-start.4
  491.3 8.2 %fusion.7 = f32[2048,1536]{1,0:T(8,128)} fusion(bf16[512,1536]{1,0:T(8,128)(2,1)S(1)} %copy-done, bf16[2048,2048]{0,1:T(8,128)(2,1)} %all-gather.5.cloned.1.call-done), kind=kOutput, calls=%fused_computation.19 | convolution fusion | flops 3221225472 | bytes 16252928 | tf_op jit(solution)/shard_map/dot_general | solution.py:73
  499.5 0.0 copy-done.4
  499.5 15.3 %add_convert_fusion = bf16[2048,1536]{1,0:T(8,128)(2,1)} fusion(f32[2048,1536]{1,0:T(8,128)} %fusion.7, bf16[1536,1536]{1,0:T(8,128)(2,1)} %param.11, bf16[2048,2048]{0,1:T(8,128)(2,1)S(1)} %copy-done.4), kind=kOutput, calls=%fused_computation.1 | convolution fusion | flops 9669967872 | bytes 29884416 | tf_op jit(solution)/shard_map/dot_general | solution.py:74
  514.8 0.0 copy-start.1
  514.8 0.0 reduce-scatter.5.cloned.1.call-update
  514.9 60.1 %reduce-scatter.5.cloned.1.call-done = bf16[256,1536]{1,0:T(8,128)(2,1)} async-done(((bf16[2048,1536]{1,0:T(8,128)(2,1)}), bf16[256,1536]{1,0:T(8,128)(2,1)}) %reduce-scatter.5.cloned.1.call-update) | async-done | bytes 786448 | tf_op jit(solution)/shard_map/reduce_scatter | solution.py:75
  575.0 0.0 copy-done.1
  575.0 2.2 fusion.13
  (4 shorter events, 0.0 us)
Async XLA Ops:
  6.5 484.7 %copy-start = (bf16[512,1536]{1,0:T(8,128)(2,1)S(1)}, bf16[512,1536]{1,0:T(8,128)(2,1)}, u32[]{:S(2)}) copy-start(bf16[512,1536]{1,0:T(8,128)(2,1)} %param.10) | copy-start | bytes 4718596
  6.5 61.2 %all-gather.3.cloned.1.call-start = ((), (), s32[]{:S(2)}) async-start(), calls=%async_computation.2 | async-start | bytes 7077888 | tf_op jit(solution)/shard_map/all_gather | solution.py:54
  24.0 297.4 %reduce-scatter.3.cloned.1.call-start = ((), (), s32[]{:S(2)}) async-start(), calls=%async_computation.3 | async-start | bytes 15728640 | tf_op jit(solution)/shard_map/reduce_scatter | solution.py:56
  109.4 381.9 %all-gather.5.cloned.1.call-start = ((), (), s32[]{:S(2)}) async-start(), calls=%async_computation.4 | async-start | bytes 10485760 | tf_op jit(solution)/shard_map/all_gather | solution.py:72
  330.2 5.8 copy-start.3
  336.0 1.9 copy-start.2
  340.4 234.5 %reduce-scatter.5.cloned.1.call-start = ((), (), s32[]{:S(2)}) async-start(), calls=%async_computation.5 | async-start | bytes 7077888 | tf_op jit(solution)/shard_map/reduce_scatter | solution.py:75
  491.3 8.2 %copy-start.4 = (bf16[2048,2048]{0,1:T(8,128)(2,1)S(1)}, bf16[2048,2048]{0,1:T(8,128)(2,1)}, u32[]{:S(2)}) copy-start(bf16[2048,2048]{0,1:T(8,128)(2,1)} %all-gather.5.cloned.1.call-done) | copy-start | bytes 25165828
  514.8 60.1 %copy-start.1 = (bf16[256,1536]{1,0:T(8,128)(2,1)S(1)}, bf16[256,1536]{1,0:T(8,128)(2,1)}, u32[]{:S(2)}) copy-start(bf16[256,1536]{1,0:T(8,128)(2,1)} %param.6) | copy-start | bytes 2359300
Sparse Core Ops, SparseCore 0:
  24.1 43.5 all-gather.2
  109.5 211.8 reduce-scatter.2
  340.6 150.6 all-gather.4
  515.0 59.9 reduce-scatter.4
where the time goes:
time: 584 us
  waiting for transfers between devices  460 us (79%)
  matrix products  53.9 us (9%)
  other arithmetic  25 us (4%)
  local copies, waits for them, and re-layouts  18 us (3%)
  blocking collectives  13.5 us (2%)
  between operations  13.3 us (2%)
    reduce_scatter x1, waiting for transfers between devices, local(): lax.psum_scatter(jnp.concatenate([jnp.dot(normed_all, w_heads, preferred_...  212 us
    all_gather x1, waiting for transfers between devices, local(): piece = lax.all_gather(hidden, 'mp', axis=0, tiled=True)  151 us
    reduce_scatter x1, waiting for transfers between devices, local(): lax.psum_scatter(partial_out.astype(jnp.bfloat16), 'dp', scatter_dimensio...  60.1 us
    all_gather x1, waiting for transfers between devices, local(): normed_all = lax.all_gather(normed, 'dp', axis=0, tiled=True)  36.9 us
    dot_general x1, matrix products, local(): jnp.dot(piece[:, head_cols:], w_down, preferred_element_type=jnp.float32)  15.3 us
    concatenate x1, other arithmetic, local(): jnp.concatenate([jnp.dot(normed_all, w_heads, preferred_element_type=jnp....  14.5 us
    dot_general x1, matrix products, local(): jnp.dot(normed_all, w_heads, preferred_element_type=jnp.float32)  13.5 us
    dot_general x1, matrix products, local(): jnp.dot(normed_all, w_up, preferred_element_type=jnp.float32)  13.5 us
  transfers between devices with their start and end apart: 4, of which 4 were waited for; matrix products, arithmetic and copies ran while one was open for 1% of the time, Pallas kernels for 0%

commit v1 on v0

v1 whole, which is shorter than its diff:
```python
import functools
import itertools

import jax
import jax.numpy as jnp
from jax import lax
from jax.experimental import pallas as pl
from jax.sharding import PartitionSpec as P


HEAD_DIM = 128
PATCHES = 256
GROUPS = 4
HOP_IN = 2
HOP_OUT = 2
GATHER = 2

EPS = 1e-06


def head_norm(values):
    mean = jnp.mean(values, axis=-1, keepdims=True)
    centered = values - mean
    spread = jnp.mean(centered * centered, axis=-1, keepdims=True)
    return centered * lax.rsqrt(spread + EPS)


def block_kernel(*refs, heads_here, head_cols, groups):
    ins, outs = refs[:groups], refs[groups:]
    piece = ins[0].shape[1]
    for s, h in itertools.product(range(2), range(heads_here)):
        first = h * HEAD_DIM
        query, keys, values = (
            jnp.concatenate(
                [r[s, :, k * head_cols + first : k * head_cols + first + HEAD_DIM] for r in ins],
                axis=0,
            )
            for k in range(3)
        )
        query = (head_norm(query.astype(jnp.float32)) * (1.0 / HEAD_DIM) ** 0.5).astype(jnp.bfloat16)
        keys = head_norm(keys.astype(jnp.float32)).astype(jnp.bfloat16)
        scores = lax.dot_general(
            query, keys, (((1,), (1,)), ((), ())), preferred_element_type=jnp.float32
        )
        weights = jnp.exp(scores)
        probs = (weights / jnp.sum(weights, axis=-1, keepdims=True)).astype(jnp.bfloat16)
        mixed = jnp.dot(probs, values, preferred_element_type=jnp.float32).astype(jnp.bfloat16)
        for g in range(groups):
            outs[g][s, :, first : first + HEAD_DIM] = mixed[g * piece : (g + 1) * piece]
    for g in range(groups):
        up = ins[g][:, :, 3 * head_cols :].astype(jnp.float32)
        outs[g][:, :, head_cols:] = jax.nn.gelu(up).astype(jnp.bfloat16)


def block(chunks, heads_here, head_cols):
    sets, rows, cols = chunks[0].shape
    return pl.pallas_call(
        functools.partial(
            block_kernel, heads_here=heads_here, head_cols=head_cols, groups=len(chunks)
        ),
        out_shape=[jax.ShapeDtypeStruct((sets, rows, cols - 2 * head_cols), jnp.bfloat16)] * len(chunks),
    )(*chunks)


def dp_bits(n_dp):
    bits = []
    bit = n_dp // 2
    while bit > 1:
        bits.append(bit)
        bit //= 2
    return bits


def swap(values, bit, n_dp):
    return lax.ppermute(values, "dp", [(i, i ^ bit) for i in range(n_dp)])


def scatter_dp(blocks, order, n_dp, me):
    live = dict(enumerate(blocks))
    for bit in order:
        low = [d for d in live if d & bit == 0]
        is_low = (me & bit) == 0
        first = jnp.stack([live[d] for d in low])
        second = jnp.stack([live[d | bit] for d in low])
        got = swap(jnp.where(is_low, second, first), bit, n_dp)
        kept = jnp.where(is_low, first, second)
        total = (kept.astype(jnp.float32) + got.astype(jnp.float32)).astype(jnp.bfloat16)
        live = {d: total[k] for k, d in enumerate(low)}
    return live[0]


def pick(position, choices):
    out = choices[0]
    for k in range(1, len(choices)):
        out = jnp.where(position == k, choices[k], out)
    return out


def local(tokens, norm_gain, w_qkv, w_up, w_attn_out, w_down):
    n_mp = lax.axis_size("mp")
    n_dp = lax.axis_size("dp")
    z = lax.axis_index("mp")
    me = lax.axis_index("dp")
    rows_here, feat_here = tokens.shape
    head_cols = w_qkv.shape[2]
    heads_here = head_cols // HEAD_DIM
    width = feat_here * n_mp
    own_images = rows_here // PATCHES
    images = own_images * n_dp
    half = images // 2
    piece = PATCHES // GROUPS
    core = me % 2
    half_cols = feat_here // 2
    bits = dp_bits(n_dp)
    order, order_b = [1] + bits, [1] + bits[::-1]

    def swap_cores(values):
        return lax.ppermute(values, "dp", [(i, i ^ 1) for i in range(n_dp)])

    def along(values, hops, way):
        pairs = []
        for d in range(n_dp):
            for p in hops:
                up = (d % 2 == 1) == (way > 0)
                source, target = (p, p + 1) if up else (n_mp - 1 - p, n_mp - 2 - p)
                pairs.append((d * n_mp + source, d * n_mp + target))
        return lax.ppermute(values, ("dp", "mp"), pairs)

    tokens_f = tokens.astype(jnp.float32)
    total, squares = lax.psum(
        (jnp.sum(tokens_f, axis=1), jnp.sum(tokens_f * tokens_f, axis=1)), "mp"
    )
    mean = total / width
    spread = squares / width - mean * mean
    normed = ((tokens_f - mean[:, None]) * lax.rsqrt(spread + EPS)[:, None] * norm_gain[None, :]).astype(jnp.bfloat16)
    normed = normed.reshape(own_images, PATCHES, feat_here)

    w_in = jnp.concatenate([w_qkv.reshape(feat_here, 3 * head_cols), w_up], axis=1)

    partial = []
    for g in range(GROUPS):
        if g % GATHER == 0:
            rows = normed[:, g * piece : (g + GATHER) * piece]
            wide = lax.all_gather(rows, "dp", axis=0, tiled=True)
        every = wide[:, g % GATHER * piece : (g % GATHER + 1) * piece]
        every = every.reshape(images * piece, feat_here)
        if g:
            every, _ = lax.optimization_barrier((every, partial[g - 2] if g > 1 else sent))
        term = jnp.dot(every, w_in, preferred_element_type=jnp.float32).astype(jnp.bfloat16)
        term = term.reshape(2, half, piece, -1)
        kept = jnp.where(core == 0, term[0], term[1])
        sent = jnp.where(core == 0, term[1], term[0])
        other = swap_cores(sent)
        partial.append(jnp.stack([kept, other], axis=1))

    count = GROUPS * half
    spans = [(c // half, c % half) for c in range(count)]

    def chunk(c):
        g, i = spans[min(max(c, 0), count - 1)]
        return partial[g][i]

    position = jnp.where(core == 0, n_mp - 1 - z, z)
    got = {}
    final = []
    last = HOP_IN * (n_mp - 1)
    for t in range(count + last):
        reach = min(n_mp, t // HOP_IN + 1)
        sums = pick(position, [chunk(t - HOP_IN * p) for p in range(reach)])
        if t >= HOP_IN:
            came, _ = lax.optimization_barrier((got[t - HOP_IN], before))
            sums = sums.astype(jnp.float32) + came.astype(jnp.float32)
            sums = sums.astype(jnp.bfloat16)
        before = sums
        if t >= last:
            final.append(sums)
        if t < count + last - HOP_IN:
            hops = [p for p in range(n_mp - 1) if 0 <= t - HOP_IN * p < count]
            got[t] = along(sums, hops, 1)

    own = [None] * count
    for i in range(half):
        made = block([final[g * half + i] for g in range(GROUPS)], heads_here, head_cols)
        for g in range(GROUPS):
            own[g * half + i] = made[g]

    position = jnp.where(core == 0, z, n_mp - 1 - z)
    passed = []
    for t in range(count + HOP_OUT * (n_mp - 2)):
        mine = own[min(t, count - 1)]
        if t >= HOP_OUT:
            mine = jnp.where(position == 0, mine, passed[t - HOP_OUT])
        hops = [p for p in range(n_mp - 1) if 0 <= t - HOP_OUT * p < count]
        passed.append(along(mine, hops, -1))

    pieces = []
    for g in range(GROUPS):
        rows = []
        for i in range(half):
            c = g * half + i
            rows.append(
                pick(position, [own[c]] + [passed[c + HOP_OUT * (p - 1)] for p in range(1, n_mp)])
            )
        rows = jnp.stack(rows)
        kept = rows[:, 0]
        other = swap_cores(rows[:, 1])
        hidden = jnp.concatenate(
            [jnp.where(core == 0, kept, other), jnp.where(core == 0, other, kept)], axis=0
        ).reshape(images * piece, -1)
        result = jnp.dot(hidden[:, :head_cols], w_attn_out, preferred_element_type=jnp.float32)
        result = result + jnp.dot(hidden[:, head_cols:], w_down, preferred_element_type=jnp.float32)
        result = result.astype(jnp.bfloat16).reshape(n_dp, own_images, piece, feat_here)
        left = scatter_dp([result[d, ..., :half_cols] for d in range(n_dp)], order, n_dp, me)
        right = scatter_dp([result[d, ..., half_cols:] for d in range(n_dp)], order_b, n_dp, me)
        pieces.append(jnp.concatenate([left, right], axis=-1))
    summed = jnp.concatenate(pieces, axis=1).reshape(rows_here, feat_here).astype(jnp.float32)
    return (tokens_f + summed).astype(jnp.bfloat16)


def solution(mesh):
    placed = (
        P("dp", "mp"),
        P("mp"),
        P("mp", None, "dp"),
        P("mp", "dp"),
        P("dp", "mp"),
        P("dp", "mp"),
    )

    return jax.shard_map(
        local, mesh=mesh, in_specs=placed, out_specs=P("dp", "mp"), check_vma=False
    )
```

time: 584 us -> 483 us (0.83)
  the two profiles are of different devices: /device:TPU:0 before, /device:TPU:28 now
where the time goes in v1:
time: 483 us; the launch traced here: 473 us
  waiting for transfers between devices  179 us (37%)
  starting transfers between devices  117 us (24%)
  matrix products  53.8 us (11%)
  other arithmetic  49.1 us (10%)
  Pallas kernels  26.7 us (6%)
  local copies, waits for them, and re-layouts  23.1 us (5%)
  between operations  15.8 us (3%)
  blocking collectives  8.16 us (2%)
    ppermute x40, waiting for transfers between devices, along(): return lax.ppermute(values, ('dp', 'mp'), pairs)  140 us
    ppermute x40, starting transfers between devices, along(): return lax.ppermute(values, ('dp', 'mp'), pairs)  93.1 us
    dot_general x4, matrix products, local(): jnp.dot(every, w_in, preferred_element_type=jnp.float32)  39.4 us
    pallas_call x4, Pallas kernels, block(): pl.pallas_call(functools.partial(block_kernel, heads_here=heads_here, hea...  26.7 us
    all_gather x2, waiting for transfers between devices, local(): wide = lax.all_gather(rows, 'dp', axis=0, tiled=True)  24.5 us
    ppermute x24, starting transfers between devices, swap(): return lax.ppermute(values, 'dp', [(i, i ^ bit) for i in range(n_dp)])  22.2 us
    convert_element_type x20, other arithmetic, local(): sums = sums.astype(jnp.bfloat16)  19.6 us
    unnamed x132, local copies, waits for them, and re-layouts  15.3 us
  transfers between devices with their start and end apart: 74, of which 41 were waited for; matrix products, arithmetic and copies ran while one was open for 25% of the time, Pallas kernels for 6%

profile of v1, /device:TPU:28, one launch (start us, length us, event | category | flops | bytes accessed | tf_op | source)
XLA Modules:
  0.0 473.3 jit_solution(12669972441462729439)
XLA Ops:
  8.1 8.2 %all-reduce = (f32[256]{0:T(256)S(1)}, f32[256]{0:T(256)S(1)}) all-reduce(f32[256]{0:T(256)S(1)} %get-tuple-element.84, f32[256]{0:T(256)S(1)} %get-tuple-element.83), channel_id=1, replica_groups=mesh['dp'=8,'mp'=4] {'mp'}, use_global_device_ids=true, to_apply=%region_3.4 | all-reduce | flops 512 | bytes 4096 | tf_op jit(solution)/shard_map/psum | solution.py:130
  19.5 6.6 %copy.150 = bf16[1536,3,512]{0,2,1:T(8,128)(2,1)} copy(bf16[1536,3,512]{2,0,1:T(8,128)(2,1)} %param.8) | data formatting | bytes 9437184 | tf_op args[2]
  26.1 6.6 %copy.151 = bf16[1536,1536]{0,1:T(8,128)(2,1)} copy(bf16[1536,1536]{1,0:T(8,128)(2,1)} %param.9) | data formatting | bytes 9437184 | tf_op args[3]
  32.7 19.9 %all-gather.3.cloned.1.call-done = bf16[8,128,1536]{2,1,0:T(8,128)(2,1)} async-done(((bf16[1,128,1536]{2,1,0:T(8,128)(2,1)}), bf16[8,128,1536]{2,1,0:T(8,128)(2,1)}) %all-gather.3.cloned.1.call-update) | async-done | bytes 3145744 | tf_op jit(solution)/shard_map/all_gather | solution.py:144
  56.2 9.7 %convolution_convert_fusion.3 = bf16[512,3072]{1,0:T(8,128)(2,1)} fusion(bf16[512,1536]{1,0:T(8,128)(2,1)} %bitcast.296, bf16[1536,1536]{0,1:T(8,128)(2,1)} %copy.151, bf16[1536,1536]{0,1:T(8,128)(2,1)S(1)} %bitcast.279), kind=kOutput, calls=%fused_computation.22 | convolution fusion | flops 4852285440 | bytes 14155776 | tf_op jit(solution)/shard_map/dot_general | solution.py:149
  65.8 3.8 broadcast_select_fusion.6
  69.9 8.7 %convolution_convert_fusion.2 = bf16[512,3072]{1,0:T(8,128)(2,1)} fusion(bf16[512,1536]{1,0:T(8,128)(2,1)S(1)} %bitcast.295, bf16[1536,1536]{0,1:T(8,128)(2,1)S(1)} %bitcast.282, bf16[1536,1536]{0,1:T(8,128)(2,1)S(1)} %bitcast.280), kind=kOutput, calls=%fused_computation.21 | convolution fusion | flops 4852285440 | bytes 14155776 | tf_op jit(solution)/shard_map/dot_general | solution.py:149
  82.2 4.6 all-gather.5.cloned.1.call-done
  93.1 10.5 %convolution_convert_fusion = bf16[512,3072]{1,0:T(8,128)(2,1)} fusion(bf16[512,1536]{1,0:T(8,128)(2,1)S(1)} %bitcast.294, bf16[1536,1536]{0,1:T(8,128)(2,1)} %copy.151, bf16[1536,1536]{0,1:T(8,128)(2,1)} %bitcast.277), kind=kOutput, calls=%fused_computation.19 | convolution fusion | flops 4852285440 | bytes 14155776 | tf_op jit(solution)/shard_map/dot_general | solution.py:149
  108.2 10.5 %convolution_convert_fusion.1 = bf16[512,3072]{1,0:T(8,128)(2,1)} fusion(bf16[512,1536]{1,0:T(8,128)(2,1)S(1)} %bitcast.293, bf16[1536,1536]{0,1:T(8,128)(2,1)} %copy.151, bf16[1536,1536]{0,1:T(8,128)(2,1)} %bitcast.278), kind=kOutput, calls=%fused_computation.20 | convolution fusion | flops 4852285440 | bytes 14155776 | tf_op jit(solution)/shard_map/dot_general | solution.py:149
  124.5 4.6 collective-permute-start.5
  132.9 4.4 collective-permute-start.9
  141.1 4.4 collective-permute-start.8
  149.6 4.4 collective-permute-start.11
  157.0 4.4 collective-permute-start.10
  161.4 3.7 collective-permute-done.11
  165.4 4.4 collective-permute-start.14
  169.9 3.7 collective-permute-done.10
  173.9 4.9 %collective-permute-start.13 = (bf16[2,64,3072]{2,1,0:T(8,128)(2,1)S(1)}, bf16[2,64,3072]{2,1,0:T(8,128)(2,1)S(1)}, u32[]{:S(2)}, u32[]{:S(2)}) collective-permute-start(bf16[2,64,3072]{2,1,0:T(8,128)(2,1)S(1)} %get-tuple-element.97.refs_1_), channel_id=1, source_target_pairs={{3,2},{2,1},{1,0},{4,5},{5,6},{6,7},{11,10},{10,9},{9,8},{12,13},{... | collective-permute-start | bytes 2359304 | tf_op jit(solution)/shard_map/ppermute | solution.py:127
  182.3 4.4 collective-permute-start.16
  186.7 3.7 collective-permute-done.13
  190.7 4.4 collective-permute-start.15
  195.2 3.6 collective-permute-done.16
  199.2 4.4 collective-permute-start.18
  203.6 3.6 collective-permute-done.15
  207.6 4.4 collective-permute-start.17
  212.0 3.6 collective-permute-done.18
  216.0 4.4 collective-permute-start.20
  225.5 7.0 %collective-permute-done.20 = bf16[2,64,3072]{2,1,0:T(8,128)(2,1)S(1)} collective-permute-done((bf16[2,64,3072]{2,1,0:T(8,128)(2,1)S(1)}, bf16[2,64,3072]{2,1,0:T(8,128)(2,1)S(1)}, u32[]{:S(2)}, u32[]{:S(2)}) %collective-permute-start.20) | collective-permute-done | bytes 786464 | tf_op jit(solution)/shard_map/ppermute | solution.py:127
  239.5 6.7 %shard_map.66 = (bf16[2,64,2048]{2,1,0:T(8,128)(2,1)}, bf16[2,64,2048]{2,1,0:T(8,128)(2,1)}, bf16[2,64,2048]{2,1,0:T(8,128)(2,1)}, bf16[2,64,2048]{2,1,0:T(8,128)(2,1)}) custom-call(bf16[2,64,3072]{2,1,0:T(8,128)(2,1)} %copy-done.8, bf16[2,64,3072]{2,1,0:T(8,128)(2,1)} %copy-done.12, bf16[2,64,3072]{2,1,0:T(8,128)(2,1)} %copy-done.14, ...), custom_call_target="tpu_custom_call" | custom-call | tf_op jit(solution)/shard_map/pallas_call | solution.py:57
  246.2 6.7 %shard_map.64 = (bf16[2,64,2048]{2,1,0:T(8,128)(2,1)}, bf16[2,64,2048]{2,1,0:T(8,128)(2,1)}, bf16[2,64,2048]{2,1,0:T(8,128)(2,1)}, bf16[2,64,2048]{2,1,0:T(8,128)(2,1)}) custom-call(bf16[2,64,3072]{2,1,0:T(8,128)(2,1)} %copy-done.6, bf16[2,64,3072]{2,1,0:T(8,128)(2,1)} %copy-done.10, bf16[2,64,3072]{2,1,0:T(8,128)(2,1)} %copy-done.13, ...), custom_call_target="tpu_custom_call" | custom-call | tf_op jit(solution)/shard_map/pallas_call | solution.py:57
  260.6 6.7 %shard_map.67 = (bf16[2,64,2048]{2,1,0:T(8,128)(2,1)}, bf16[2,64,2048]{2,1,0:T(8,128)(2,1)}, bf16[2,64,2048]{2,1,0:T(8,128)(2,1)}, bf16[2,64,2048]{2,1,0:T(8,128)(2,1)}) custom-call(bf16[2,64,3072]{2,1,0:T(8,128)(2,1)} %copy-done.7, bf16[2,64,3072]{2,1,0:T(8,128)(2,1)} %copy-done.11, bf16[2,64,3072]{2,1,0:T(8,128)(2,1)} %copy-done.17, ...), custom_call_target="tpu_custom_call" | custom-call | tf_op jit(solution)/shard_map/pallas_call | solution.py:57
  269.3 6.7 %shard_map.65 = (bf16[2,64,2048]{2,1,0:T(8,128)(2,1)}, bf16[2,64,2048]{2,1,0:T(8,128)(2,1)}, bf16[2,64,2048]{2,1,0:T(8,128)(2,1)}, bf16[2,64,2048]{2,1,0:T(8,128)(2,1)}) custom-call(bf16[2,64,3072]{2,1,0:T(8,128)(2,1)} %copy-done.5, bf16[2,64,3072]{2,1,0:T(8,128)(2,1)} %copy-done.9, bf16[2,64,3072]{2,1,0:T(8,128)(2,1)} %copy-done.18, ...), custom_call_target="tpu_custom_call" | custom-call | tf_op jit(solution)/shard_map/pallas_call | solution.py:57
  280.9 21.4 %collective-permute-done.29 = bf16[2,64,2048]{2,1,0:T(8,128)(2,1)S(1)} collective-permute-done((bf16[2,64,2048]{2,1,0:T(8,128)(2,1)S(1)}, bf16[2,64,2048]{2,1,0:T(8,128)(2,1)S(1)}, u32[]{:S(2)}, u32[]{:S(2)}) %collective-permute-start.29) | collective-permute-done | bytes 524320 | tf_op jit(solution)/shard_map/ppermute | solution.py:127
  303.9 8.3 %collective-permute-done.25 = bf16[2,64,2048]{2,1,0:T(8,128)(2,1)S(1)} collective-permute-done((bf16[2,64,2048]{2,1,0:T(8,128)(2,1)S(1)}, bf16[2,64,2048]{2,1,0:T(8,128)(2,1)S(1)}, u32[]{:S(2)}, u32[]{:S(2)}) %collective-permute-start.25) | collective-permute-done | bytes 524320 | tf_op jit(solution)/shard_map/ppermute | solution.py:127
  313.7 4.1 collective-permute-done.31
  319.3 5.1 %collective-permute-done.30 = bf16[2,64,2048]{2,1,0:T(8,128)(2,1)S(1)} collective-permute-done((bf16[2,64,2048]{2,1,0:T(8,128)(2,1)S(1)}, bf16[2,64,2048]{2,1,0:T(8,128)(2,1)S(1)}, u32[]{:S(2)}, u32[]{:S(2)}) %collective-permute-start.30) | collective-permute-done | bytes 524320 | tf_op jit(solution)/shard_map/ppermute | solution.py:127
  326.0 4.1 collective-permute-done.40
  331.6 4.1 collective-permute-done.39
  337.2 4.1 collective-permute-done.42
  342.9 4.1 collective-permute-done.41
  348.4 4.3 collective-permute-done.51
  354.0 4.2 collective-permute-done.50
  366.1 4.5 collective-permute-done.52
  370.6 5.5 %collective-permute-done.62 = bf16[2,64,2048]{2,1,0:T(8,128)(2,1)S(1)} collective-permute-done((bf16[2,64,2048]{2,1,0:T(8,128)(2,1)}, bf16[2,64,2048]{2,1,0:T(8,128)(2,1)S(1)}, u32[]{:S(2)}, u32[]{:S(2)}) %collective-permute-start.62) | collective-permute-done | bytes 524320 | tf_op jit(solution)/shard_map/ppermute | solution.py:127
  383.2 5.2 %collective-permute-done.61 = bf16[2,64,2048]{2,1,0:T(8,128)(2,1)S(1)} collective-permute-done((bf16[2,64,2048]{2,1,0:T(8,128)(2,1)S(1)}, bf16[2,64,2048]{2,1,0:T(8,128)(2,1)S(1)}, u32[]{:S(2)}, u32[]{:S(2)}) %collective-permute-start.61) | collective-permute-done | bytes 524320 | tf_op jit(solution)/shard_map/ppermute | solution.py:127
  396.0 9.1 %collective-permute-done.63 = bf16[2,64,2048]{2,1,0:T(8,128)(2,1)S(1)} collective-permute-done((bf16[2,64,2048]{2,1,0:T(8,128)(2,1)S(1)}, bf16[2,64,2048]{2,1,0:T(8,128)(2,1)S(1)}, u32[]{:S(2)}, u32[]{:S(2)}) %collective-permute-start.63) | collective-permute-done | bytes 524320 | tf_op jit(solution)/shard_map/ppermute | solution.py:127
  453.8 3.7 collective-permute-done.67
  (376 shorter events, 167.0 us)
Async XLA Ops:
  6.5 46.1 %all-gather.3.cloned.1.call-start = ((), (), s32[]{:S(2)}) async-start(), calls=%async_computation | async-start | bytes 3538944 | tf_op jit(solution)/shard_map/all_gather | solution.py:144
  18.7 68.1 %all-gather.5.cloned.1.call-start = ((), (), s32[]{:S(2)}) async-start(), calls=%async_computation.1 | async-start | bytes 3538944 | tf_op jit(solution)/shard_map/all_gather | solution.py:144
  69.6 19.4 %collective-permute-start = (bf16[4,64,3072]{2,1,0:T(8,128)(2,1)}, bf16[4,64,3072]{2,1,0:T(8,128)(2,1)}, u32[]{:S(2)}, u32[]{:S(2)}) collective-permute-start(bf16[4,64,3072]{2,1,0:T(8,128)(2,1)} %bitcast.4), channel_id=1, source_target_pairs={{0,4},{4,0},{8,12},{12,8},{16,20},{20,16},{24,28},{28,24},{1,5},{5... | collective-permute-start | bytes 4718600 | tf_op jit(solution)/shard_map/ppermute | solution.py:118
  81.9 40.9 %collective-permute-start.1 = (bf16[4,64,3072]{2,1,0:T(8,128)(2,1)}, bf16[4,64,3072]{2,1,0:T(8,128)(2,1)}, u32[]{:S(2)}, u32[]{:S(2)}) collective-permute-start(bf16[4,64,3072]{2,1,0:T(8,128)(2,1)} %bitcast.10), channel_id=1, source_target_pairs={{0,4},{4,0},{8,12},{12,8},{16,20},{20,16},{24,28},{28,24},{1,5},{5... | collective-permute-start | bytes 4718600 | tf_op jit(solution)/shard_map/ppermute | solution.py:118
  90.4 14.6 %collective-permute-start.2 = (bf16[2,64,3072]{2,1,0:T(8,128)(2,1)S(1)}, bf16[2,64,3072]{2,1,0:T(8,128)(2,1)S(1)}, u32[]{:S(2)}, u32[]{:S(2)}) collective-permute-start(bf16[2,64,3072]{2,1,0:T(8,128)(2,1)S(1)} %get-tuple-element.133), channel_id=1, source_target_pairs={{3,2},{4,5},{11,10},{12,13},{19,18},{20,21},{27,26},{28,29}} | collective-permute-start | bytes 2359304 | tf_op jit(solution)/shard_map/ppermute | solution.py:127
  103.6 15.0 %collective-permute-start.4 = (bf16[2,64,3072]{2,1,0:T(8,128)(2,1)S(1)}, bf16[2,64,3072]{2,1,0:T(8,128)(2,1)S(1)}, u32[]{:S(2)}, u32[]{:S(2)}) collective-permute-start(bf16[2,64,3072]{2,1,0:T(8,128)(2,1)S(1)} %get-tuple-element.134), channel_id=1, source_target_pairs={{3,2},{4,5},{11,10},{12,13},{19,18},{20,21},{27,26},{28,29}} | collective-permute-start | bytes 2359304 | tf_op jit(solution)/shard_map/ppermute | solution.py:127
  106.3 16.5 %collective-permute-start.3 = (bf16[2,64,3072]{2,1,0:T(8,128)(2,1)S(1)}, bf16[2,64,3072]{2,1,0:T(8,128)(2,1)S(1)}, u32[]{:S(2)}, u32[]{:S(2)}) collective-permute-start(bf16[2,64,3072]{2,1,0:T(8,128)(2,1)S(1)} %get-tuple-element.113), channel_id=1, source_target_pairs={{3,2},{2,1},{4,5},{5,6},{11,10},{10,9},{12,13},{13,14},{19,18},{18... | collective-permute-start | bytes 2359304 | tf_op jit(solution)/shard_map/ppermute | solution.py:127
  120.0 11.4 %collective-permute-start.6 = (bf16[2,64,3072]{2,1,0:T(8,128)(2,1)S(1)}, bf16[2,64,3072]{2,1,0:T(8,128)(2,1)S(1)}, u32[]{:S(2)}, u32[]{:S(2)}) collective-permute-start(bf16[2,64,3072]{2,1,0:T(8,128)(2,1)S(1)} %get-tuple-element.111), channel_id=1, source_target_pairs={{3,2},{2,1},{4,5},{5,6},{11,10},{10,9},{12,13},{13,14},{19,18},{18... | collective-permute-start | bytes 2359304 | tf_op jit(solution)/shard_map/ppermute | solution.py:127
  124.5 15.3 %collective-permute-start.5 = (bf16[2,64,3072]{2,1,0:T(8,128)(2,1)S(1)}, bf16[2,64,3072]{2,1,0:T(8,128)(2,1)S(1)}, u32[]{:S(2)}, u32[]{:S(2)}) collective-permute-start(bf16[2,64,3072]{2,1,0:T(8,128)(2,1)S(1)} %get-tuple-element.109), channel_id=1, source_target_pairs={{3,2},{2,1},{1,0},{4,5},{5,6},{6,7},{11,10},{10,9},{9,8},{12,13},{... | collective-permute-start | bytes 2359304 | tf_op jit(solution)/shard_map/ppermute | solution.py:127
  129.6 27.1 %collective-permute-start.7 = (bf16[4,64,3072]{2,1,0:T(8,128)(2,1)S(1)}, bf16[4,64,3072]{2,1,0:T(8,128)(2,1)S(1)}, u32[]{:S(2)}, u32[]{:S(2)}) collective-permute-start(bf16[4,64,3072]{2,1,0:T(8,128)(2,1)S(1)} %bitcast.292), channel_id=1, source_target_pairs={{0,4},{4,0},{8,12},{12,8},{16,20},{20,16},{24,28},{28,24},{1,5},{5... | collective-permute-start | bytes 4718600 | tf_op jit(solution)/shard_map/ppermute | solution.py:118
  129.7 60.7 %collective-permute-start.12 = (bf16[4,64,3072]{2,1,0:T(8,128)(2,1)S(1)}, bf16[4,64,3072]{2,1,0:T(8,128)(2,1)S(1)}, u32[]{:S(2)}, u32[]{:S(2)}) collective-permute-start(bf16[4,64,3072]{2,1,0:T(8,128)(2,1)S(1)} %bitcast.291), channel_id=1, source_target_pairs={{0,4},{4,0},{8,12},{12,8},{16,20},{20,16},{24,28},{28,24},{1,5},{5... | collective-permute-start | bytes 4718600 | tf_op jit(solution)/shard_map/ppermute | solution.py:118
  132.9 15.3 %collective-permute-start.9 = (bf16[2,64,3072]{2,1,0:T(8,128)(2,1)S(1)}, bf16[2,64,3072]{2,1,0:T(8,128)(2,1)S(1)}, u32[]{:S(2)}, u32[]{:S(2)}) collective-permute-start(bf16[2,64,3072]{2,1,0:T(8,128)(2,1)S(1)} %get-tuple-element.107), channel_id=1, source_target_pairs={{3,2},{2,1},{1,0},{4,5},{5,6},{6,7},{11,10},{10,9},{9,8},{12,13},{... | collective-permute-start | bytes 2359304 | tf_op jit(solution)/shard_map/ppermute | solution.py:127
  141.1 15.5 %collective-permute-start.8 = (bf16[2,64,3072]{2,1,0:T(8,128)(2,1)S(1)}, bf16[2,64,3072]{2,1,0:T(8,128)(2,1)S(1)}, u32[]{:S(2)}, u32[]{:S(2)}) collective-permute-start(bf16[2,64,3072]{2,1,0:T(8,128)(2,1)S(1)} %get-tuple-element.105.refs_0_), channel_id=1, source_target_pairs={{3,2},{2,1},{1,0},{4,5},{5,6},{6,7},{11,10},{10,9},{9,8},{12,13},{... | collective-permute-start | bytes 2359304 | tf_op jit(solution)/shard_map/ppermute | solution.py:127
  149.6 15.5 %collective-permute-start.11 = (bf16[2,64,3072]{2,1,0:T(8,128)(2,1)S(1)}, bf16[2,64,3072]{2,1,0:T(8,128)(2,1)S(1)}, u32[]{:S(2)}, u32[]{:S(2)}) collective-permute-start(bf16[2,64,3072]{2,1,0:T(8,128)(2,1)S(1)} %get-tuple-element.103.refs_0_), channel_id=1, source_target_pairs={{3,2},{2,1},{1,0},{4,5},{5,6},{6,7},{11,10},{10,9},{9,8},{12,13},{... | collective-permute-start | bytes 2359304 | tf_op jit(solution)/shard_map/ppermute | solution.py:127
  157.0 16.5 %collective-permute-start.10 = (bf16[2,64,3072]{2,1,0:T(8,128)(2,1)S(1)}, bf16[2,64,3072]{2,1,0:T(8,128)(2,1)S(1)}, u32[]{:S(2)}, u32[]{:S(2)}) collective-permute-start(bf16[2,64,3072]{2,1,0:T(8,128)(2,1)S(1)} %get-tuple-element.101.refs_0_), channel_id=1, source_target_pairs={{3,2},{2,1},{1,0},{4,5},{5,6},{6,7},{11,10},{10,9},{9,8},{12,13},{... | collective-permute-start | bytes 2359304 | tf_op jit(solution)/shard_map/ppermute | solution.py:127
  165.4 16.5 %collective-permute-start.14 = (bf16[2,64,3072]{2,1,0:T(8,128)(2,1)S(1)}, bf16[2,64,3072]{2,1,0:T(8,128)(2,1)S(1)}, u32[]{:S(2)}, u32[]{:S(2)}) collective-permute-start(bf16[2,64,3072]{2,1,0:T(8,128)(2,1)S(1)} %get-tuple-element.99.refs_0_), channel_id=1, source_target_pairs={{3,2},{2,1},{1,0},{4,5},{5,6},{6,7},{11,10},{10,9},{9,8},{12,13},{... | collective-permute-start | bytes 2359304 | tf_op jit(solution)/shard_map/ppermute | solution.py:127
  173.9 16.5 %collective-permute-start.13 = (bf16[2,64,3072]{2,1,0:T(8,128)(2,1)S(1)}, bf16[2,64,3072]{2,1,0:T(8,128)(2,1)S(1)}, u32[]{:S(2)}, u32[]{:S(2)}) collective-permute-start(bf16[2,64,3072]{2,1,0:T(8,128)(2,1)S(1)} %get-tuple-element.97.refs_1_), channel_id=1, source_target_pairs={{3,2},{2,1},{1,0},{4,5},{5,6},{6,7},{11,10},{10,9},{9,8},{12,13},{... | collective-permute-start | bytes 2359304 | tf_op jit(solution)/shard_map/ppermute | solution.py:127
  182.3 16.5 %collective-permute-start.16 = (bf16[2,64,3072]{2,1,0:T(8,128)(2,1)S(1)}, bf16[2,64,3072]{2,1,0:T(8,128)(2,1)S(1)}, u32[]{:S(2)}, u32[]{:S(2)}) collective-permute-start(bf16[2,64,3072]{2,1,0:T(8,128)(2,1)S(1)} %get-tuple-element.95.refs_1_), channel_id=1, source_target_pairs={{3,2},{2,1},{1,0},{4,5},{5,6},{6,7},{11,10},{10,9},{9,8},{12,13},{... | collective-permute-start | bytes 2359304 | tf_op jit(solution)/shard_map/ppermute | solution.py:127
  190.7 16.5 %collective-permute-start.15 = (bf16[2,64,3072]{2,1,0:T(8,128)(2,1)S(1)}, bf16[2,64,3072]{2,1,0:T(8,128)(2,1)S(1)}, u32[]{:S(2)}, u32[]{:S(2)}) collective-permute-start(bf16[2,64,3072]{2,1,0:T(8,128)(2,1)S(1)} %get-tuple-element.93.refs_1_), channel_id=1, source_target_pairs={{3,2},{2,1},{1,0},{4,5},{5,6},{6,7},{11,10},{10,9},{9,8},{12,13},{... | collective-permute-start | bytes 2359304 | tf_op jit(solution)/shard_map/ppermute | solution.py:127
  199.2 16.5 %collective-permute-start.18 = (bf16[2,64,3072]{2,1,0:T(8,128)(2,1)S(1)}, bf16[2,64,3072]{2,1,0:T(8,128)(2,1)S(1)}, u32[]{:S(2)}, u32[]{:S(2)}) collective-permute-start(bf16[2,64,3072]{2,1,0:T(8,128)(2,1)S(1)} %get-tuple-element.91.refs_1_), channel_id=1, source_target_pairs={{3,2},{2,1},{1,0},{4,5},{5,6},{6,7},{11,10},{10,9},{9,8},{12,13},{... | collective-permute-start | bytes 2359304 | tf_op jit(solution)/shard_map/ppermute | solution.py:127
  207.6 16.5 %collective-permute-start.17 = (bf16[2,64,3072]{2,1,0:T(8,128)(2,1)S(1)}, bf16[2,64,3072]{2,1,0:T(8,128)(2,1)S(1)}, u32[]{:S(2)}, u32[]{:S(2)}) collective-permute-start(bf16[2,64,3072]{2,1,0:T(8,128)(2,1)S(1)} %get-tuple-element.89.refs_2_), channel_id=1, source_target_pairs={{3,2},{2,1},{1,0},{4,5},{5,6},{6,7},{11,10},{10,9},{9,8},{12,13},{... | collective-permute-start | bytes 2359304 | tf_op jit(solution)/shard_map/ppermute | solution.py:127
  216.0 16.5 %collective-permute-start.20 = (bf16[2,64,3072]{2,1,0:T(8,128)(2,1)S(1)}, bf16[2,64,3072]{2,1,0:T(8,128)(2,1)S(1)}, u32[]{:S(2)}, u32[]{:S(2)}) collective-permute-start(bf16[2,64,3072]{2,1,0:T(8,128)(2,1)S(1)} %get-tuple-element.87.refs_2_), channel_id=1, source_target_pairs={{3,2},{2,1},{1,0},{4,5},{5,6},{6,7},{11,10},{10,9},{9,8},{12,13},{... | collective-permute-start | bytes 2359304 | tf_op jit(solution)/shard_map/ppermute | solution.py:127
  235.1 20.9 %collective-permute-start.21 = (bf16[2,64,3072]{2,1,0:T(8,128)(2,1)}, bf16[2,64,3072]{2,1,0:T(8,128)(2,1)}, u32[]{:S(2)}, u32[]{:S(2)}) collective-permute-start(bf16[2,64,3072]{2,1,0:T(8,128)(2,1)} %add_convert_fusion.3.refs_3_), channel_id=1, source_target_pairs={{1,0},{6,7},{9,8},{14,15},{17,16},{22,23},{25,24},{30,31}} | collective-permute-start | bytes 2359304 | tf_op jit(solution)/shard_map/ppermute | solution.py:127
  237.9 20.4 %collective-permute-start.26 = (bf16[2,64,3072]{2,1,0:T(8,128)(2,1)}, bf16[2,64,3072]{2,1,0:T(8,128)(2,1)}, u32[]{:S(2)}, u32[]{:S(2)}) collective-permute-start(bf16[2,64,3072]{2,1,0:T(8,128)(2,1)} %add_convert_fusion.2.refs_3_), channel_id=1, source_target_pairs={{1,0},{6,7},{9,8},{14,15},{17,16},{22,23},{25,24},{30,31}} | collective-permute-start | bytes 2359304 | tf_op jit(solution)/shard_map/ppermute | solution.py:127
  252.9 14.4 %collective-permute-start.27 = (bf16[2,64,2048]{2,1,0:T(8,128)(2,1)}, bf16[2,64,2048]{2,1,0:T(8,128)(2,1)}, u32[]{:S(2)}, u32[]{:S(2)}) collective-permute-start(bf16[2,64,2048]{2,1,0:T(8,128)(2,1)} %get-tuple-element.72), channel_id=1, source_target_pairs={{0,1},{7,6},{8,9},{15,14},{16,17},{23,22},{24,25},{31,30}} | collective-permute-start | bytes 1572872 | tf_op jit(solution)/shard_map/ppermute | solution.py:127
  254.4 21.6 %collective-permute-start.23 = (bf16[2,64,2048]{2,1,0:T(8,128)(2,1)}, bf16[2,64,2048]{2,1,0:T(8,128)(2,1)}, u32[]{:S(2)}, u32[]{:S(2)}) collective-permute-start(bf16[2,64,2048]{2,1,0:T(8,128)(2,1)} %get-tuple-element.68), channel_id=1, source_target_pairs={{0,1},{7,6},{8,9},{15,14},{16,17},{23,22},{24,25},{31,30}} | collective-permute-start | bytes 1572872 | tf_op jit(solution)/shard_map/ppermute | solution.py:127
  278.0 24.4 %collective-permute-start.29 = (bf16[2,64,2048]{2,1,0:T(8,128)(2,1)S(1)}, bf16[2,64,2048]{2,1,0:T(8,128)(2,1)S(1)}, u32[]{:S(2)}, u32[]{:S(2)}) collective-permute-start(bf16[2,64,2048]{2,1,0:T(8,128)(2,1)S(1)} %broadcast_select_fusion.30), channel_id=1, source_target_pairs={{0,1},{1,2},{2,3},{7,6},{6,5},{5,4},{8,9},{9,10},{10,11},{15,14},{... | collective-permute-start | bytes 1572872 | tf_op jit(solution)/shard_map/ppermute | solution.py:127
  279.5 32.7 %collective-permute-start.25 = (bf16[2,64,2048]{2,1,0:T(8,128)(2,1)S(1)}, bf16[2,64,2048]{2,1,0:T(8,128)(2,1)S(1)}, u32[]{:S(2)}, u32[]{:S(2)}) collective-permute-start(bf16[2,64,2048]{2,1,0:T(8,128)(2,1)S(1)} %broadcast_select_fusion.32), channel_id=1, source_target_pairs={{0,1},{1,2},{2,3},{7,6},{6,5},{5,4},{8,9},{9,10},{10,11},{15,14},{... | collective-permute-start | bytes 1572872 | tf_op jit(solution)/shard_map/ppermute | solution.py:127
  302.5 15.4 %collective-permute-start.31 = (bf16[2,64,2048]{2,1,0:T(8,128)(2,1)S(1)}, bf16[2,64,2048]{2,1,0:T(8,128)(2,1)S(1)}, u32[]{:S(2)}, u32[]{:S(2)}) collective-permute-start(bf16[2,64,2048]{2,1,0:T(8,128)(2,1)S(1)} %broadcast_select_fusion.28), channel_id=1, source_target_pairs={{0,1},{1,2},{2,3},{7,6},{6,5},{5,4},{8,9},{9,10},{10,11},{15,14},{... | collective-permute-start | bytes 1572872 | tf_op jit(solution)/shard_map/ppermute | solution.py:127
  312.3 12.2 %collective-permute-start.30 = (bf16[2,64,2048]{2,1,0:T(8,128)(2,1)S(1)}, bf16[2,64,2048]{2,1,0:T(8,128)(2,1)S(1)}, u32[]{:S(2)}, u32[]{:S(2)}) collective-permute-start(bf16[2,64,2048]{2,1,0:T(8,128)(2,1)S(1)} %broadcast_select_fusion.29), channel_id=1, source_target_pairs={{0,1},{1,2},{2,3},{7,6},{6,5},{5,4},{8,9},{9,10},{10,11},{15,14},{... | collective-permute-start | bytes 1572872 | tf_op jit(solution)/shard_map/ppermute | solution.py:127
  317.9 12.2 %collective-permute-start.40 = (bf16[2,64,2048]{2,1,0:T(8,128)(2,1)S(1)}, bf16[2,64,2048]{2,1,0:T(8,128)(2,1)S(1)}, u32[]{:S(2)}, u32[]{:S(2)}) collective-permute-start(bf16[2,64,2048]{2,1,0:T(8,128)(2,1)S(1)} %broadcast_select_fusion.26), channel_id=1, source_target_pairs={{0,1},{1,2},{2,3},{7,6},{6,5},{5,4},{8,9},{9,10},{10,11},{15,14},{... | collective-permute-start | bytes 1572872 | tf_op jit(solution)/shard_map/ppermute | solution.py:127
  324.5 11.2 %collective-permute-start.39 = (bf16[2,64,2048]{2,1,0:T(8,128)(2,1)S(1)}, bf16[2,64,2048]{2,1,0:T(8,128)(2,1)S(1)}, u32[]{:S(2)}, u32[]{:S(2)}) collective-permute-start(bf16[2,64,2048]{2,1,0:T(8,128)(2,1)S(1)} %broadcast_select_fusion.27), channel_id=1, source_target_pairs={{0,1},{1,2},{2,3},{7,6},{6,5},{5,4},{8,9},{9,10},{10,11},{15,14},{... | collective-permute-start | bytes 1572872 | tf_op jit(solution)/shard_map/ppermute | solution.py:127
  330.2 11.2 %collective-permute-start.42 = (bf16[2,64,2048]{2,1,0:T(8,128)(2,1)S(1)}, bf16[2,64,2048]{2,1,0:T(8,128)(2,1)S(1)}, u32[]{:S(2)}, u32[]{:S(2)}) collective-permute-start(bf16[2,64,2048]{2,1,0:T(8,128)(2,1)S(1)} %broadcast_select_fusion.24), channel_id=1, source_target_pairs={{0,1},{1,2},{2,3},{7,6},{6,5},{5,4},{8,9},{9,10},{10,11},{15,14},{... | collective-permute-start | bytes 1572872 | tf_op jit(solution)/shard_map/ppermute | solution.py:127
  335.8 11.2 %collective-permute-start.41 = (bf16[2,64,2048]{2,1,0:T(8,128)(2,1)S(1)}, bf16[2,64,2048]{2,1,0:T(8,128)(2,1)S(1)}, u32[]{:S(2)}, u32[]{:S(2)}) collective-permute-start(bf16[2,64,2048]{2,1,0:T(8,128)(2,1)S(1)} %broadcast_select_fusion.25), channel_id=1, source_target_pairs={{0,1},{1,2},{2,3},{7,6},{6,5},{5,4},{8,9},{9,10},{10,11},{15,14},{... | collective-permute-start | bytes 1572872 | tf_op jit(solution)/shard_map/ppermute | solution.py:127
  341.4 11.2 %collective-permute-start.51 = (bf16[2,64,2048]{2,1,0:T(8,128)(2,1)S(1)}, bf16[2,64,2048]{2,1,0:T(8,128)(2,1)S(1)}, u32[]{:S(2)}, u32[]{:S(2)}) collective-permute-start(bf16[2,64,2048]{2,1,0:T(8,128)(2,1)S(1)} %broadcast_select_fusion.22), channel_id=1, source_target_pairs={{0,1},{1,2},{2,3},{7,6},{6,5},{5,4},{8,9},{9,10},{10,11},{15,14},{... | collective-permute-start | bytes 1572872 | tf_op jit(solution)/shard_map/ppermute | solution.py:127
  347.1 11.2 %collective-permute-start.50 = (bf16[2,64,2048]{2,1,0:T(8,128)(2,1)S(1)}, bf16[2,64,2048]{2,1,0:T(8,128)(2,1)S(1)}, u32[]{:S(2)}, u32[]{:S(2)}) collective-permute-start(bf16[2,64,2048]{2,1,0:T(8,128)(2,1)S(1)} %broadcast_select_fusion.23), channel_id=1, source_target_pairs={{0,1},{1,2},{2,3},{7,6},{6,5},{5,4},{8,9},{9,10},{10,11},{15,14},{... | collective-permute-start | bytes 1572872 | tf_op jit(solution)/shard_map/ppermute | solution.py:127
  352.7 11.2 %collective-permute-start.53 = (bf16[2,64,2048]{2,1,0:T(8,128)(2,1)S(1)}, bf16[2,64,2048]{2,1,0:T(8,128)(2,1)S(1)}, u32[]{:S(2)}, u32[]{:S(2)}) collective-permute-start(bf16[2,64,2048]{2,1,0:T(8,128)(2,1)S(1)} %broadcast_select_fusion.20), channel_id=1, source_target_pairs={{0,1},{1,2},{2,3},{7,6},{6,5},{5,4},{8,9},{9,10},{10,11},{15,14},{... | collective-permute-start | bytes 1572872 | tf_op jit(solution)/shard_map/ppermute | solution.py:127
  359.2 11.4 %collective-permute-start.52 = (bf16[2,64,2048]{2,1,0:T(8,128)(2,1)}, bf16[2,64,2048]{2,1,0:T(8,128)(2,1)}, u32[]{:S(2)}, u32[]{:S(2)}) collective-permute-start(bf16[2,64,2048]{2,1,0:T(8,128)(2,1)} %broadcast_select_fusion.21), channel_id=1, source_target_pairs={{0,1},{1,2},{2,3},{7,6},{6,5},{5,4},{8,9},{9,10},{10,11},{15,14},{... | collective-permute-start | bytes 1572872 | tf_op jit(solution)/shard_map/ppermute | solution.py:127
  364.8 11.3 %collective-permute-start.62 = (bf16[2,64,2048]{2,1,0:T(8,128)(2,1)}, bf16[2,64,2048]{2,1,0:T(8,128)(2,1)S(1)}, u32[]{:S(2)}, u32[]{:S(2)}) collective-permute-start(bf16[2,64,2048]{2,1,0:T(8,128)(2,1)} %broadcast_select_fusion.18), channel_id=1, source_target_pairs={{1,2},{2,3},{6,5},{5,4},{9,10},{10,11},{14,13},{13,12},{17,18},{18... | collective-permute-start | bytes 1572872 | tf_op jit(solution)/shard_map/ppermute | solution.py:127
  377.2 11.1 %collective-permute-start.61 = (bf16[2,64,2048]{2,1,0:T(8,128)(2,1)S(1)}, bf16[2,64,2048]{2,1,0:T(8,128)(2,1)S(1)}, u32[]{:S(2)}, u32[]{:S(2)}) collective-permute-start(bf16[2,64,2048]{2,1,0:T(8,128)(2,1)S(1)} %get-tuple-element.219), channel_id=1, source_target_pairs={{1,2},{2,3},{6,5},{5,4},{9,10},{10,11},{14,13},{13,12},{17,18},{18... | collective-permute-start | bytes 1572872 | tf_op jit(solution)/shard_map/ppermute | solution.py:127
  378.7 15.3 %collective-permute-start.64 = (bf16[2,64,2048]{2,1,0:T(8,128)(2,1)S(1)}, bf16[2,64,2048]{2,1,0:T(8,128)(2,1)S(1)}, u32[]{:S(2)}, u32[]{:S(2)}) collective-permute-start(bf16[2,64,2048]{2,1,0:T(8,128)(2,1)S(1)} %get-tuple-element.220), channel_id=1, source_target_pairs={{2,3},{5,4},{10,11},{13,12},{18,19},{21,20},{26,27},{29,28}} | collective-permute-start | bytes 1572872 | tf_op jit(solution)/shard_map/ppermute | solution.py:127
  390.4 15.4 %collective-permute-start.32 = (bf16[4,64,2048]{2,1,0:T(8,128)(2,1)S(1)}, bf16[4,64,2048]{2,1,0:T(8,128)(2,1)S(1)}, u32[]{:S(2)}, u32[]{:S(2)}) collective-permute-start(bf16[4,64,2048]{2,1,0:T(8,128)(2,1)S(1)} %slice_bitcast_fusion.6), channel_id=1, source_target_pairs={{0,4},{4,0},{8,12},{12,8},{16,20},{20,16},{24,28},{28,24},{1,5},{5... | collective-permute-start | bytes 3145736 | tf_op jit(solution)/shard_map/ppermute | solution.py:118
  390.8 21.7 %collective-permute-start.43 = (bf16[4,64,2048]{2,1,0:T(8,128)(2,1)S(1)}, bf16[4,64,2048]{2,1,0:T(8,128)(2,1)S(1)}, u32[]{:S(2)}, u32[]{:S(2)}) collective-permute-start(bf16[4,64,2048]{2,1,0:T(8,128)(2,1)S(1)} %slice_bitcast_fusion.4), channel_id=1, source_target_pairs={{0,4},{4,0},{8,12},{12,8},{16,20},{20,16},{24,28},{28,24},{1,5},{5... | collective-permute-start | bytes 3145736 | tf_op jit(solution)/shard_map/ppermute | solution.py:118
  396.0 21.0 %collective-permute-start.54 = (bf16[4,64,2048]{2,1,0:T(8,128)(2,1)S(1)}, bf16[4,64,2048]{2,1,0:T(8,128)(2,1)S(1)}, u32[]{:S(2)}, u32[]{:S(2)}) collective-permute-start(bf16[4,64,2048]{2,1,0:T(8,128)(2,1)S(1)} %slice_bitcast_fusion.2), channel_id=1, source_target_pairs={{0,4},{4,0},{8,12},{12,8},{16,20},{20,16},{24,28},{28,24},{1,5},{5... | collective-permute-start | bytes 3145736 | tf_op jit(solution)/shard_map/ppermute | solution.py:118
  405.7 22.5 %collective-permute-start.65 = (bf16[4,64,2048]{2,1,0:T(8,128)(2,1)S(1)}, bf16[4,64,2048]{2,1,0:T(8,128)(2,1)S(1)}, u32[]{:S(2)}, u32[]{:S(2)}) collective-permute-start(bf16[4,64,2048]{2,1,0:T(8,128)(2,1)S(1)} %slice_bitcast_fusion), channel_id=1, source_target_pairs={{0,4},{4,0},{8,12},{12,8},{16,20},{20,16},{24,28},{28,24},{1,5},{5... | collective-permute-start | bytes 3145736 | tf_op jit(solution)/shard_map/ppermute | solution.py:118
  423.9 11.3 %collective-permute-start.37 = (bf16[2,1,64,768]{3,2,1,0:T(8,128)(2,1)S(1)}, bf16[2,1,64,768]{3,2,1,0:T(8,128)(2,1)S(1)}, u32[]{:S(2)}, u32[]{:S(2)}) collective-permute-start(bf16[2,1,64,768]{3,2,1,0:T(8,128)(2,1)S(1)} %broadcast_select_fusion.45), channel_id=1, source_target_pairs={{0,8},{4,12},{8,0},{12,4},{16,24},{20,28},{24,16},{28,20},{1,9},{5... | collective-permute-start | bytes 589832 | tf_op jit(solution)/shard_map/ppermute | solution.py:75
  435.2 15.3 %collective-permute-start.66 = (bf16[4,1,64,768]{3,2,1,0:T(8,128)(2,1)S(1)}, bf16[4,1,64,768]{3,2,1,0:T(8,128)(2,1)S(1)}, u32[]{:S(2)}, u32[]{:S(2)}) collective-permute-start(bf16[4,1,64,768]{3,2,1,0:T(8,128)(2,1)S(1)} %broadcast_select_fusion.35), channel_id=1, source_target_pairs={{0,4},{4,0},{8,12},{12,8},{16,20},{20,16},{24,28},{28,24},{1,5},{5... | collective-permute-start | bytes 1179656 | tf_op jit(solution)/shard_map/ppermute | solution.py:75
  435.4 17.9 %collective-permute-start.69 = (bf16[4,1,64,768]{3,2,1,0:T(8,128)(2,1)S(1)}, bf16[4,1,64,768]{3,2,1,0:T(8,128)(2,1)S(1)}, u32[]{:S(2)}, u32[]{:S(2)}) collective-permute-start(bf16[4,1,64,768]{3,2,1,0:T(8,128)(2,1)S(1)} %broadcast_select_fusion.34), channel_id=1, source_target_pairs={{0,4},{4,0},{8,12},{12,8},{16,20},{20,16},{24,28},{28,24},{1,5},{5... | collective-permute-start | bytes 1179656 | tf_op jit(solution)/shard_map/ppermute | solution.py:75
  (91 other events, 1363.7 us)
Sparse Core Ops, SparseCore 0:
  18.8 33.8 all-gather.2
  54.6 32.1 all-gather.4
